TPU v7x, 32 devices: a whole 2x2x4 slice. The times are simulated.
32 devices in a mesh: dp: 4 (over x, core), tensor: 8 (over z, y).
Axes of the slice: x: 2, y: 2, z: 4, core: 2. Of those that a mesh axis runs over, the one named last changes fastest.
Arguments:
- out_grad: bfloat16 [2, 320, 4096], P(None, 'dp', 'tensor'), may hold values from -0.3125 to 0.3125
- layer_input: bfloat16 [2, 320, 4096], P(None, 'dp', 'tensor'), may hold values from -8 to 8
- w_down: bfloat16 [16384, 4096], P('tensor'), may hold values from -0.046875 to 0.046875
- silu_gate: bfloat16 [2, 320, 16384], P(None, 'dp', 'tensor'), may hold values from -6 to 6
- up_proj: bfloat16 [2, 320, 16384], P(None, 'dp', 'tensor'), may hold values from -6 to 6
- slope_codes: int32 [2, 32, 16384], P(None, 'dp', 'tensor'), may hold values from 0 to 1073741823
Outputs:
- grad_down: bfloat16 [16384, 4096], P('tensor', 'dp')
- grad_gate: bfloat16 [4096, 16384], P('dp', 'tensor')
- grad_up: bfloat16 [4096, 16384], P('dp', 'tensor')
Inputs may be any that keep to these rules, and one draw needn't show every extreme that they name: `slope_codes`: every word holds ten independent 3-bit codes; all eight codes occur.
All inputs are finite; a program needn't handle non-finite values.
Results may differ from a plain program's by a relative error of at most 0.018.
Values may be sent and summed in bfloat16 or wider, within the bound.
A program may use at most 128 MiB of HBM per device.

v0:
```python
import jax
import jax.numpy as jnp
from jax import lax
from jax.sharding import PartitionSpec as P

SLOPE_LEVELS = (-0.09, 0.06, 0.22, 0.41, 0.6, 0.79, 0.96, 1.08)


def decode_slopes(packed):
    shifts = 3 * jnp.arange(10, dtype=jnp.int32)
    pieces = jnp.bitwise_and(jnp.right_shift(packed[..., None, :], shifts[:, None]), 7)
    pieces = pieces.reshape(packed.shape[:-2] + (packed.shape[-2] * 10, packed.shape[-1]))
    result = jnp.full(pieces.shape, SLOPE_LEVELS[0], jnp.float32)
    for symbol in range(1, 8):
        result = jnp.where(pieces == symbol, jnp.float32(SLOPE_LEVELS[symbol]), result)
    return result


def shards(out_grad, layer_input, w_down, silu_gate, up_proj, slope_codes):
    micro_count = out_grad.shape[0]
    model_width = w_down.shape[1]
    hidden_width = w_down.shape[0]
    group_rows = micro_count * out_grad.shape[1]
    grad_rows, input_rows = (
        lax.all_gather(out_grad, "tensor", axis=2, tiled=True),
        lax.all_gather(layer_input, "tensor", axis=2, tiled=True),
    )
    output_all = grad_rows.reshape(-1, model_width)
    input_all = input_rows.reshape(-1, model_width)
    gate_act = silu_gate.reshape(-1, hidden_width).astype(jnp.float32)
    up_value = up_proj.reshape(-1, hidden_width).astype(jnp.float32)
    hidden = (gate_act * up_value).astype(jnp.bfloat16)
    slopes = decode_slopes(slope_codes).reshape(-1, hidden_width)
    hidden_grad = lax.dot_general(
        output_all, w_down, (((1,), (1,)), ((), ())), preferred_element_type=jnp.float32
    )
    up_grad = (hidden_grad * gate_act).astype(jnp.bfloat16)
    gate_grad = (hidden_grad * up_value * slopes).astype(jnp.bfloat16)
    block_inputs, block_outputs = (
        lax.all_to_all(input_all, "dp", split_axis=1, concat_axis=0, tiled=True),
        lax.all_to_all(output_all, "dp", split_axis=1, concat_axis=0, tiled=True),
    )
    activations = jnp.concatenate((gate_grad, up_grad, hidden), axis=1)
    values = lax.all_gather(activations, "dp", axis=0, tiled=True)
    row_count = values.shape[0]
    groups = row_count // group_rows
    inputs_3d = block_inputs.reshape(groups, group_rows, block_inputs.shape[1])
    outputs_3d = block_outputs.reshape(groups, group_rows, block_outputs.shape[1])
    values_3d = values.reshape(groups, group_rows, values.shape[1])
    gate_up_parts = jnp.einsum(
        "grd,grf->gdf",
        inputs_3d,
        values_3d[:, :, : 2 * hidden_width],
        preferred_element_type=jnp.float32,
    )
    down_parts = jnp.einsum(
        "grf,grd->gfd",
        values_3d[:, :, 2 * hidden_width :],
        outputs_3d,
        preferred_element_type=jnp.float32,
    )
    gate_up_sum = jnp.sum(gate_up_parts.astype(jnp.bfloat16).astype(jnp.float32), axis=0)
    down_sum = jnp.sum(down_parts.astype(jnp.bfloat16).astype(jnp.float32), axis=0)
    grad_down = down_sum.astype(jnp.bfloat16)
    grad_gate = gate_up_sum[:, :hidden_width].astype(jnp.bfloat16)
    grad_up = gate_up_sum[:, hidden_width:].astype(jnp.bfloat16)
    return (grad_down, grad_gate, grad_up)


def solution(mesh):
    return jax.shard_map(
        shards,
        mesh=mesh,
        in_specs=(
            P(None, "dp", "tensor"),
            P(None, "dp", "tensor"),
            P("tensor", None),
            P(None, "dp", "tensor"),
            P(None, "dp", "tensor"),
            P(None, "dp", "tensor"),
        ),
        out_specs=(P("tensor", "dp"), P("dp", "tensor"), P("dp", "tensor")),
        check_vma=False,
    )
```

profile of v0, /device:TPU:0, one launch (start us, length us, event | category | flops | bytes accessed | tf_op | source)
XLA Modules:
  0.0 234.2 jit_solution(13841438188736707465)
XLA Ops:
  7.2 0.7 all-gather.4.cloned.1.call-update
  7.9 0.7 all-gather.8.cloned.1.call-update
  8.6 0.0 all-gather.6.cloned.1.call-start
  8.7 0.1 shift_right_arithmetic.28
  8.8 0.1 shift_right_arithmetic.30
  8.9 1.1 shift_right_arithmetic.25
  10.0 0.2 shift_right_arithmetic.26
  10.2 44.1 %all-gather.4.cloned.1.call-done = bf16[2,80,4096]{2,1,0:T(8,128)(2,1)} async-done(((bf16[2,80,512]{2,1,0:T(8,128)(2,1)}), bf16[2,80,4096]{2,1,0:T(8,128)(2,1)}) %all-gather.4.cloned.1.call-update) | async-done | bytes 1310736 | tf_op jit(solution)/shard_map/all_gather | solution.py:25
  54.3 12.8 %fusion.4 = (bf16[160,2048]{1,0:T(8,128)(2,1)S(1)}, bf16[160,2048]{1,0:T(8,128)(2,1)S(1)}, bf16[160,2048]{1,0:T(8,128)(2,1)S(1)}) fusion(s32[160,2048]{1,0:T(8,128)S(1)} %shift_right_arithmetic.26, bf16[2,80,2048]{2,1,0:T(8,128)(2,1)} %param.10, s32[160]{0:T(256)S(1)} %shift_right_arithmetic.30, bf16[2,80,2048]{2,1,0:T(8,128)(2,1)} %param.9, ...), kind=kOutput, calls=%fused_computation.10 | convolution fusion | flops 2692546560 | bytes 22676096 | tf_op jit(solution)/shard_map/dot_general | solution.py:34
  67.1 1.4 pad_maximum_fusion
  68.5 27.8 %all-gather.8.cloned.1.call-done = bf16[2,80,4096]{2,1,0:T(8,128)(2,1)} async-done(((bf16[2,80,512]{2,1,0:T(8,128)(2,1)}), bf16[2,80,4096]{2,1,0:T(8,128)(2,1)}) %all-gather.8.cloned.1.call-update) | async-done | bytes 1310736 | tf_op jit(solution)/shard_map/all_gather | solution.py:26
  96.3 3.2 %all_to_all.27 = bf16[160,4,1024]{2,1,0:T(4,128)(2,1)S(1)} reshape(bf16[2,80,4096]{2,1,0:T(8,128)(2,1)} %all-gather.8.cloned.1.call-done) | data formatting | bytes 2621440 | tf_op jit(solution)/shard_map/all_to_all | solution.py:40
  99.5 1.4 copy.12
  101.0 4.5 %all-to-all-start.1 = ((bf16[160,4,1024]{2,0,1:T(8,128)(2,1)}), bf16[160,4,1024]{2,0,1:T(8,128)(2,1)}, u32[]{:S(2)}, u32[]{:S(2)}) async-start(bf16[160,4,1024]{2,0,1:T(8,128)(2,1)} %copy.12), calls=%async_computation.1 | async-start | bytes 2621440 | tf_op jit(solution)/shard_map/all_to_all | solution.py:40
  105.5 1.0 all_to_all.24
  106.5 1.5 copy.11
  108.0 29.0 %all-to-all-done.1 = bf16[160,4,1024]{2,0,1:T(8,128)(2,1)} async-done(((bf16[160,4,1024]{2,0,1:T(8,128)(2,1)}), bf16[160,4,1024]{2,0,1:T(8,128)(2,1)}, u32[]{:S(2)}, u32[]{:S(2)}) %all-to-all-start.1) | async-done | bytes 1310752 | tf_op jit(solution)/shard_map/all_to_all | solution.py:40
  137.0 3.7 %all-to-all-start = ((bf16[160,4,1024]{2,0,1:T(8,128)(2,1)}), bf16[160,4,1024]{2,0,1:T(8,128)(2,1)S(1)}, u32[]{:S(2)}, u32[]{:S(2)}) async-start(bf16[160,4,1024]{2,0,1:T(8,128)(2,1)} %copy.11), calls=%async_computation | async-start | bytes 2621440 | tf_op jit(solution)/shard_map/all_to_all | solution.py:41
  140.8 39.4 %all-gather.6.cloned.1.call-done = bf16[640,6144]{1,0:T(8,128)(2,1)} async-done(((bf16[160,6144]{1,0:T(8,128)(2,1)}), bf16[640,6144]{1,0:T(8,128)(2,1)}) %all-gather.6.cloned.1.call-update) | async-done | bytes 7864336 | tf_op jit(solution)/shard_map/all_gather | solution.py:44
  180.2 19.0 %convert_reduce_fusion = bf16[4096,1024]{1,0:T(8,128)(2,1)} fusion(bf16[4,160,6144]{2,1,0:T(8,128)(2,1)} %bitcast.21, bf16[160,4,1024]{2,0,1:T(8,128)(2,1)} %all-to-all-done.1), kind=kOutput, calls=%fused_computation | convolution fusion | flops 5398069248 | bytes 14942208 | tf_op jit(solution)/shard_map/grd,grf->gdf/dot_general | solution.py:50
  199.2 6.0 %fusion.8 = (bf16[1024,2048]{0,1:T(8,128)(2,1)}, bf16[1024,2048]{0,1:T(8,128)(2,1)}) fusion(bf16[1024,4096]{0,1:T(8,128)(2,1)} %bitcast.19), kind=kLoop, calls=%fused_computation.16 | loop fusion | bytes 16777216 | tf_op jit(solution)/shard_map/slice | solution.py:66
  205.2 6.4 %copy.14 = bf16[1024,2048]{1,0:T(8,128)(2,1)} copy(bf16[1024,2048]{0,1:T(8,128)(2,1)} %get-tuple-element.6) | data formatting | bytes 8388608
  211.6 6.4 %copy.13 = bf16[1024,2048]{1,0:T(8,128)(2,1)} copy(bf16[1024,2048]{0,1:T(8,128)(2,1)} %get-tuple-element.7) | data formatting | bytes 8388608
  218.0 9.6 %convert_reduce_fusion.1 = bf16[2048,1024]{1,0:T(8,128)(2,1)} fusion(bf16[4,160,6144]{2,1,0:T(8,128)(2,1)} %bitcast.22, bf16[160,4,1024]{2,0,1:T(8,128)(2,1)S(1)} %all-to-all-done), kind=kOutput, calls=%fused_computation.1 | convolution fusion | flops 2699034624 | bytes 8126464 | tf_op jit(solution)/shard_map/grf,grd->gfd/dot_general | solution.py:56
  (9 shorter events, 0.1 us)
Async XLA Ops:
  7.2 47.2 %all-gather.4.cloned.1.call-start = ((), (), s32[]{:S(2)}) async-start(), calls=%async_computation.2 | async-start | bytes 1474560 | tf_op jit(solution)/shard_map/all_gather | solution.py:25
  7.9 88.4 %all-gather.8.cloned.1.call-start = ((), (), s32[]{:S(2)}) async-start(), calls=%async_computation.4 | async-start | bytes 1474560 | tf_op jit(solution)/shard_map/all_gather | solution.py:26
  8.6 171.5 %all-gather.6.cloned.1.call-start = ((), (), s32[]{:S(2)}) async-start(), calls=%async_computation.3 | async-start | bytes 9830400 | tf_op jit(solution)/shard_map/all_gather | solution.py:44
  101.0 4.5 %copy-start = (bf16[2,80,4096]{2,1,0:T(8,128)(2,1)S(1)}, bf16[2,80,4096]{2,1,0:T(8,128)(2,1)}, u32[]{:S(2)}) copy-start(bf16[2,80,4096]{2,1,0:T(8,128)(2,1)} %all-gather.4.cloned.1.call-done) | copy-start | bytes 3932164
  101.0 36.0 %all-to-all-start.1 = ((bf16[160,4,1024]{2,0,1:T(8,128)(2,1)}), bf16[160,4,1024]{2,0,1:T(8,128)(2,1)}, u32[]{:S(2)}, u32[]{:S(2)}) async-start(bf16[160,4,1024]{2,0,1:T(8,128)(2,1)} %copy.12), calls=%async_computation.1 | async-start | bytes 2621440 | tf_op jit(solution)/shard_map/all_to_all | solution.py:40
  137.0 81.0 %all-to-all-start = ((bf16[160,4,1024]{2,0,1:T(8,128)(2,1)}), bf16[160,4,1024]{2,0,1:T(8,128)(2,1)S(1)}, u32[]{:S(2)}, u32[]{:S(2)}) async-start(bf16[160,4,1024]{2,0,1:T(8,128)(2,1)} %copy.11), calls=%async_computation | async-start | bytes 2621440 | tf_op jit(solution)/shard_map/all_to_all | solution.py:41
Sparse Core Ops, SparseCore 0:
  10.0 44.2 all-gather.3
  56.4 39.8 all-gather.7
  98.4 81.6 all-gather.5
where the time goes:
time: 235 us; the launch traced here: 234 us
  waiting for transfers between devices  142 us (60%)
  matrix products  41.4 us (18%)
  local copies, waits for them, and re-layouts  27.5 us (12%)
  between operations  13.8 us (6%)
  starting transfers between devices  8.34 us (4%)
    all_gather x1, waiting for transfers between devices, shards(): lax.all_gather(out_grad, 'tensor', axis=2, tiled=True)  44.1 us
    all_gather x1, waiting for transfers between devices, shards(): values = lax.all_gather(activations, 'dp', axis=0, tiled=True)  39.4 us
    all_to_all x1, waiting for transfers between devices, shards(): lax.all_to_all(input_all, 'dp', split_axis=1, concat_axis=0, tiled=True)  29 us
    all_gather x1, waiting for transfers between devices, shards(): lax.all_gather(layer_input, 'tensor', axis=2, tiled=True)  27.8 us
    dot_general x1, matrix products, shards(): jnp.einsum('grd,grf->gdf', inputs_3d, values_3d[:, :, :2 * hidden_width],...  19 us
    unnamed x4, local copies, waits for them, and re-layouts  12.8 us
    dot_general x1, matrix products, shards(): lax.dot_general(output_all, w_down, (((1,), (1,)), ((), ())), preferred_e...  12.8 us
    dot_general x1, matrix products, shards(): jnp.einsum('grf,grd->gfd', values_3d[:, :, 2 * hidden_width:], outputs_3d...  9.61 us
  transfers between devices with their start and end apart: 5, of which 4 were waited for; matrix products, arithmetic and copies ran while one was open for 24% of the time, Pallas kernels for 0%

commit v1 on v0

--- a/solution.py
+++ b/solution.py
@@ -4,6 +4,12 @@
 from jax.sharding import PartitionSpec as P
 
 SLOPE_LEVELS = (-0.09, 0.06, 0.22, 0.41, 0.6, 0.79, 0.96, 1.08)
+
+
+def swap_blocks(array, name, split, join):
+    parts = jnp.split(array, lax.axis_size(name), axis=split)
+    received = lax.all_to_all(jnp.stack(parts), name, 0, 0)
+    return jnp.concatenate(received, axis=join)
 
 
 def decode_slopes(packed):
@@ -37,7 +43,7 @@
     up_grad = (hidden_grad * gate_act).astype(jnp.bfloat16)
     gate_grad = (hidden_grad * up_value * slopes).astype(jnp.bfloat16)
     block_inputs, block_outputs = (
-        lax.all_to_all(input_all, "dp", split_axis=1, concat_axis=0, tiled=True),
+        swap_blocks(input_all, "dp", 1, 0),
         lax.all_to_all(output_all, "dp", split_axis=1, concat_axis=0, tiled=True),
     )
     activations = jnp.concatenate((gate_grad, up_grad, hidden), axis=1)

time: 235 us -> 228 us (0.970)
  local copies, waits for them, and re-layouts: 27.5 us -> 11.5 us
  matrix products: 41.4 us -> 49.1 us
    unnamed x4 -> x2, local copies, waits for them, and re-layouts: 12.8 us -> 0.01 us
    dot_general x1, matrix products: 19 us -> 26.8 us  [shards(): jnp.einsum('grd,grf->gdf', inputs_3d, values_3d[:, :, :2 * hidden_width],...]
    all_to_all x2 -> x0, local copies, waits for them, and re-layouts: 4.67 us -> none  [shards(): lax.all_to_all(input_all, 'dp', split_axis=1, concat_axis=0, tiled=True)]
  transfers between devices with their start and end apart: 5 -> 5, of which waited for: 4 -> 4; matrix products, arithmetic and copies ran while one was open for 24% -> 23% of each run, Pallas kernels for 0% -> 0%
where the time goes in v1:
time: 228 us
  waiting for transfers between devices  142 us (62%)
  matrix products  49.1 us (22%)
  between operations  13.8 us (6%)
  local copies, waits for them, and re-layouts  11.5 us (5%)
  starting transfers between devices  8.27 us (4%)
  other arithmetic  2.63 us (1%)
    all_gather x1, waiting for transfers between devices, shards(): lax.all_gather(out_grad, 'tensor', axis=2, tiled=True)  44.1 us
    all_gather x1, waiting for transfers between devices, shards(): values = lax.all_gather(activations, 'dp', axis=0, tiled=True)  41.2 us
    all_gather x1, waiting for transfers between devices, shards(): lax.all_gather(layer_input, 'tensor', axis=2, tiled=True)  27.8 us
    all_to_all x1, waiting for transfers between devices, swap_blocks(): received = lax.all_to_all(jnp.stack(parts), name, 0, 0)  27.7 us
    dot_general x1, matrix products, shards(): jnp.einsum('grd,grf->gdf', inputs_3d, values_3d[:, :, :2 * hidden_width],...  26.8 us
    dot_general x1, matrix products, shards(): lax.dot_general(output_all, w_down, (((1,), (1,)), ((), ())), preferred_e...  12.8 us
    dot_general x1, matrix products, shards(): jnp.einsum('grf,grd->gfd', values_3d[:, :, 2 * hidden_width:], outputs_3d...  9.61 us
    slice x1, local copies, waits for them, and re-layouts, shards(): grad_up = gate_up_sum[:, hidden_width:].astype(jnp.bfloat16)  6.14 us
  transfers between devices with their start and end apart: 5, of which 4 were waited for; matrix products, arithmetic and copies ran while one was open for 23% of the time, Pallas kernels for 0%

profile of v1, /device:TPU:0, one launch (start us, length us, event | category | flops | bytes accessed | tf_op | source)
XLA Modules:
  0.0 227.5 jit_solution(3306116674054740505)
XLA Ops:
  7.2 0.0 all-gather.4.cloned.1.call-start
  7.2 0.7 all-gather.4.cloned.1.call-update
  7.9 0.0 all-gather.8.cloned.1.call-start
  7.9 0.7 all-gather.8.cloned.1.call-update
  8.6 0.0 all-gather.6.cloned.1.call-start
  8.7 0.1 shift_right_arithmetic.28
  8.8 0.1 shift_right_arithmetic.30
  8.9 1.1 shift_right_arithmetic.25
  10.0 0.2 shift_right_arithmetic.26
  10.2 44.1 %all-gather.4.cloned.1.call-done = bf16[2,80,4096]{2,1,0:T(8,128)(2,1)} async-done(((bf16[2,80,512]{2,1,0:T(8,128)(2,1)}), bf16[2,80,4096]{2,1,0:T(8,128)(2,1)}) %all-gather.4.cloned.1.call-update) | async-done | bytes 1310736 | tf_op jit(solution)/shard_map/all_gather | solution.py:31
  54.3 12.8 %fusion.4 = (bf16[160,2048]{1,0:T(8,128)(2,1)S(1)}, bf16[160,2048]{1,0:T(8,128)(2,1)S(1)}, bf16[160,2048]{1,0:T(8,128)(2,1)S(1)}) fusion(s32[160,2048]{1,0:T(8,128)S(1)} %shift_right_arithmetic.26, bf16[2,80,2048]{2,1,0:T(8,128)(2,1)} %param.10, s32[160]{0:T(256)S(1)} %shift_right_arithmetic.30, bf16[2,80,2048]{2,1,0:T(8,128)(2,1)} %param.9, ...), kind=kOutput, calls=%fused_computation.10 | convolution fusion | flops 2692546560 | bytes 22676096 | tf_op jit(solution)/shard_map/dot_general | solution.py:40
  67.1 1.4 pad_maximum_fusion
  68.5 27.8 %all-gather.8.cloned.1.call-done = bf16[2,80,4096]{2,1,0:T(8,128)(2,1)} async-done(((bf16[2,80,512]{2,1,0:T(8,128)(2,1)}), bf16[2,80,4096]{2,1,0:T(8,128)(2,1)}) %all-gather.8.cloned.1.call-update) | async-done | bytes 1310736 | tf_op jit(solution)/shard_map/all_gather | solution.py:32
  96.3 1.4 slice_bitcast_fusion.3
  97.7 1.2 pad_maximum_fusion.1
  98.9 4.4 %all-to-all-start.1 = ((bf16[4,160,1024]{2,1,0:T(8,128)(2,1)}), bf16[4,160,1024]{2,1,0:T(8,128)(2,1)}, u32[]{:S(2)}, u32[]{:S(2)}) async-start(bf16[4,160,1024]{2,1,0:T(8,128)(2,1)} %pad_maximum_fusion.1), calls=%async_computation.1 | async-start | bytes 2621440 | tf_op jit(solution)/shard_map/all_to_all | solution.py:11
  103.3 1.0 all_to_all.15
  104.4 1.4 copy.9
  105.8 27.7 %all-to-all-done.1 = bf16[4,160,1024]{2,1,0:T(8,128)(2,1)} async-done(((bf16[4,160,1024]{2,1,0:T(8,128)(2,1)}), bf16[4,160,1024]{2,1,0:T(8,128)(2,1)}, u32[]{:S(2)}, u32[]{:S(2)}) %all-to-all-start.1) | async-done | bytes 1310752 | tf_op jit(solution)/shard_map/all_to_all | solution.py:11
  133.5 3.7 %all-to-all-start = ((bf16[160,4,1024]{2,0,1:T(8,128)(2,1)}), bf16[160,4,1024]{2,0,1:T(8,128)(2,1)S(1)}, u32[]{:S(2)}, u32[]{:S(2)}) async-start(bf16[160,4,1024]{2,0,1:T(8,128)(2,1)} %copy.9), calls=%async_computation | async-start | bytes 2621440 | tf_op jit(solution)/shard_map/all_to_all | solution.py:47
  137.2 41.2 %all-gather.6.cloned.1.call-done = bf16[640,6144]{1,0:T(8,128)(2,1)} async-done(((bf16[160,6144]{1,0:T(8,128)(2,1)}), bf16[640,6144]{1,0:T(8,128)(2,1)}) %all-gather.6.cloned.1.call-update) | async-done | bytes 7864336 | tf_op jit(solution)/shard_map/all_gather | solution.py:50
  178.5 26.8 %convert_reduce_fusion = bf16[1024,4096]{1,0:T(8,128)(2,1)} fusion(bf16[4,160,1024]{2,1,0:T(8,128)(2,1)} %all-to-all-done.1, bf16[4,160,6144]{2,1,0:T(8,128)(2,1)} %bitcast.27), kind=kOutput, calls=%fused_computation | convolution fusion | flops 5398069248 | bytes 14942208 | tf_op jit(solution)/shard_map/grd,grf->gdf/dot_general | solution.py:56
  205.3 6.1 %fusion.7 = (bf16[1024,2048]{1,0:T(8,128)(2,1)}, bf16[1024,2048]{1,0:T(8,128)(2,1)}) fusion(bf16[1024,4096]{1,0:T(8,128)(2,1)} %convert_reduce_fusion), kind=kLoop, calls=%fused_computation.20 | loop fusion | bytes 16777216 | tf_op jit(solution)/shard_map/slice | solution.py:72
  211.4 9.6 %convert_reduce_fusion.1 = bf16[2048,1024]{1,0:T(8,128)(2,1)} fusion(bf16[4,160,6144]{2,1,0:T(8,128)(2,1)} %bitcast.28, bf16[160,4,1024]{2,0,1:T(8,128)(2,1)S(1)} %all-to-all-done), kind=kOutput, calls=%fused_computation.1 | convolution fusion | flops 2699034624 | bytes 8126464 | tf_op jit(solution)/shard_map/grf,grd->gfd/dot_general | solution.py:62
  (7 shorter events, 0.0 us)
Async XLA Ops:
  7.2 47.2 %all-gather.4.cloned.1.call-start = ((), (), s32[]{:S(2)}) async-start(), calls=%async_computation.2 | async-start | bytes 1474560 | tf_op jit(solution)/shard_map/all_gather | solution.py:31
  7.9 88.4 %all-gather.8.cloned.1.call-start = ((), (), s32[]{:S(2)}) async-start(), calls=%async_computation.4 | async-start | bytes 1474560 | tf_op jit(solution)/shard_map/all_gather | solution.py:32
  8.6 169.8 %all-gather.6.cloned.1.call-start = ((), (), s32[]{:S(2)}) async-start(), calls=%async_computation.3 | async-start | bytes 9830400 | tf_op jit(solution)/shard_map/all_gather | solution.py:50
  98.9 4.4 %copy-start = (bf16[2,80,4096]{2,1,0:T(8,128)(2,1)S(1)}, bf16[2,80,4096]{2,1,0:T(8,128)(2,1)}, u32[]{:S(2)}) copy-start(bf16[2,80,4096]{2,1,0:T(8,128)(2,1)} %all-gather.4.cloned.1.call-done) | copy-start | bytes 3932164
  98.9 34.6 %all-to-all-start.1 = ((bf16[4,160,1024]{2,1,0:T(8,128)(2,1)}), bf16[4,160,1024]{2,1,0:T(8,128)(2,1)}, u32[]{:S(2)}, u32[]{:S(2)}) async-start(bf16[4,160,1024]{2,1,0:T(8,128)(2,1)} %pad_maximum_fusion.1), calls=%async_computation.1 | async-start | bytes 2621440 | tf_op jit(solution)/shard_map/all_to_all | solution.py:11
  133.5 77.9 %all-to-all-start = ((bf16[160,4,1024]{2,0,1:T(8,128)(2,1)}), bf16[160,4,1024]{2,0,1:T(8,128)(2,1)S(1)}, u32[]{:S(2)}, u32[]{:S(2)}) async-start(bf16[160,4,1024]{2,0,1:T(8,128)(2,1)} %copy.9), calls=%async_computation | async-start | bytes 2621440 | tf_op jit(solution)/shard_map/all_to_all | solution.py:47
Sparse Core Ops, SparseCore 0:
  10.0 44.2 all-gather.3
  56.4 39.8 all-gather.7
  98.4 79.9 all-gather.5
